TPU v7x, 32 devices: a whole 2x2x4 slice. The times are simulated.
32 devices in a mesh: dp: 8 (over z, y), expert: 4 (over x, core).
Axes of the slice: x: 2, y: 2, z: 4, core: 2. Of those that a mesh axis runs over, the one named last changes fastest.
Arguments:
- tokens: bfloat16 [1024, 4096], P('dp'), may hold values from -6 to 6
- expert_ids: int32 [1024, 2], P('dp'), may hold values from 0 to 3, all different within a row; in each aligned block of 128 rows (0 to 127, 128 to 255, ...) at most 96 rows name the same one
- gate_weights: float32 [1024, 2], P('dp'), may hold values from 0.2 to 1
- live_counts: int32 [8], P('dp'), may hold values from 64 to 128, as said below
- w_gate: bfloat16 [4, 4096, 8192], P('expert', None, 'dp'), may hold values from -0.09375 to 0.09375
- w_up: bfloat16 [4, 4096, 8192], P('expert', None, 'dp'), may hold values from -0.09375 to 0.09375
- w_down: bfloat16 [4, 8192, 4096], P('expert', 'dp'), may hold values from -0.0625 to 0.0625
Outputs:
- mixed: bfloat16 [1024, 4096], P('dp')
- total_loads: int32 [4], replicated
Inputs may be any that keep to these rules, and one draw needn't show every extreme that they name: `expert_ids`: each token names two different experts. Among the tokens of one rank no expert is named more than 96 times, a bound that some block reaches in some ranks. Rank r's first live_counts[r] tokens are live, the rest are padding. Some rank has all 128 tokens live.
All inputs are finite; a program needn't handle non-finite values.
Results may differ from a plain program's by a relative error of at most 0.017.
Values may be sent and summed in bfloat16 or wider, within the bound.
A program may use at most 128 MiB of HBM per device.

v0:
```python
import functools

import jax
import jax.numpy as jnp
from jax import lax
from jax.experimental import pallas as pl
from jax.experimental.pallas import tpu as pltpu
from jax.sharding import PartitionSpec as P

MESH = pl.DeviceIdType.MESH
BF16, F32 = jnp.bfloat16, jnp.float32


def routing_weights(expert_ids, gate_weights, live_total, n_experts, my_expert):
    live = (jnp.arange(expert_ids.shape[0], dtype=jnp.int32) < live_total)[:, None]
    mine = (expert_ids == my_expert) & live
    weight = jnp.sum(jnp.where(mine, gate_weights, 0.0), axis=1)
    named = (expert_ids[:, :, None] == jnp.arange(n_experts, dtype=jnp.int32)) & live[:, :, None]
    return weight, jnp.sum(named.astype(jnp.int32), axis=(0, 1))


def general(tokens, expert_ids, gate_weights, live_counts, w_gate, w_up, w_down):
    weight, loads = routing_weights(
        expert_ids, gate_weights, live_counts[0], lax.axis_size("expert"), lax.axis_index("expert")
    )
    rows = lax.all_gather(tokens, "dp", axis=0, tiled=True)
    scale = lax.all_gather(weight, "dp", axis=0, tiled=True)[:, None]
    gate_act = jnp.dot(rows, w_gate[0], preferred_element_type=F32)
    up_act = jnp.dot(rows, w_up[0], preferred_element_type=F32)
    hidden = (jax.nn.silu(gate_act) * up_act * scale).astype(BF16)
    partial = jnp.dot(hidden, w_down[0], preferred_element_type=F32).astype(BF16)
    summed = lax.psum_scatter(partial, "dp", scatter_dimension=0, tiled=True)
    return lax.psum(summed, "expert"), lax.psum(loads, "dp")


def kernel(n_y, n_planes, tokens, meta, w_gate, w_up, w_down, out, meta_out,
           G, M, WG, WU, WD, H, Y, RC, RY0, RX0, RX1, RY1, RZ, OUT, send_sem, recv_sem, local_sem):
    dp, ex = lax.axis_index("dp"), lax.axis_index("expert")
    z, y = dp // n_y, dp % n_y
    x, c = ex // 2, ex % 2
    yo, xo, co = 1 - y, 1 - x, 1 - c
    n_dp = n_y * n_planes
    pieces, rows, width = G.shape[1:]
    half, quarter = pieces // 2, pieces // 4

    def xor(a, k):
        lo, hi = a % 2, a // 2
        lo = lo if k % 2 == 0 else 1 - lo
        hi = hi if k // 2 == 0 else hi + 1 - 2 * (hi % 2)
        return hi * 2 + lo

    plane = [xor(z, k) for k in range(n_planes)]
    y_peer, x_peer, core_peer = (z * n_y + yo, ex), (dp, xo * 2 + c), (dp, x * 2 + co)
    z_peer = [(plane[k] * n_y + y, ex) for k in range(n_planes)]
    me = dp
    rank = [plane[k] * n_y + y for k in range(n_planes)]
    other = [plane[k] * n_y + yo for k in range(n_planes)]
    pair = [pl.ds(plane[k] * n_y, n_y) for k in range(n_planes)]

    peers = [(lax.rem(dp + d, n_dp), ex) for d in range(1, n_dp)] + [x_peer, core_peer]
    barrier = pltpu.get_barrier_semaphore()

    n_local = [0]

    def local(src, dst):
        copy = pltpu.make_async_copy(src, dst, local_sem.at[n_local[0]])
        n_local[0] += 1
        copy.start()
        return copy

    own_loads = [local(tokens.at[:, pl.ds(q * width, width)], G.at[me, q]) for q in range(pieces)]
    own_meta = local(meta, M.at[me])
    weight_loads = [local(w_gate.at[0], WG), local(w_up.at[0], WU), local(w_down.at[0], WD)]

    for a, b in peers:
        pl.semaphore_signal(barrier, inc=1, device_id={"dp": a, "expert": b}, device_id_type=MESH)
    pl.semaphore_wait(barrier, len(peers))

    sent = []

    def send(src, dst, to):
        i = len(sent)
        copy = pltpu.make_async_remote_copy(
            src_ref=src, dst_ref=dst, send_sem=send_sem.at[i], recv_sem=recv_sem.at[i],
            device_id={"dp": to[0], "expert": to[1]}, device_id_type=MESH,
        )
        copy.start()
        sent.append(copy)
        return copy

    def got(*copies):
        for copy in copies:
            copy.wait_recv()

    mine_x = pl.ds(c * half + x * quarter, quarter)
    mine_c, other_c = pl.ds(c * half, half), pl.ds(co * half, half)

    def piece(xh, o):
        return c * half + xh * quarter + o

    for copy in own_loads:
        copy.wait()
    own_meta.wait()

    ZS = [None] + [send(G.at[me, mine_x], G.at[me, mine_x], z_peer[k]) for k in range(1, n_planes)]
    A0 = send(G.at[me, mine_x], G.at[me, mine_x], y_peer)
    metas = [send(M.at[me], M.at[me], (lax.rem(dp + d, n_dp), ex)) for d in range(1, n_dp)]

    def stage_a(k):
        got(ZS[k])
        ref = G.at[rank[k], piece(x, 0)]
        ref1 = G.at[rank[k], piece(x, 1)]
        return send(ref, ref, x_peer), send(ref1, ref1, y_peer)

    def stage_b(k, a):
        got(a[0])
        first = [G.at[rank[k], piece(h, 0)] for h in range(2)]
        b = [send(ref, ref, y_peer) for ref in first]
        got(a[1])
        ref = G.at[pair[k], piece(x, 1)]
        return b + [send(ref, ref, x_peer)]

    def stage_d(k, b):
        got(*b)
        ref = G.at[pair[k], mine_c]
        return send(ref, ref, core_peer)

    h_tile = min(256, WG.shape[1])

    def gate_up(k):
        columns = [jnp.transpose(M[plane[k] * n_y + j])[:, 0:1] for j in range(n_y)]
        scale = jnp.concatenate(columns, axis=0)

        def tile(t, carry):
            cols = pl.ds(pl.multiple_of(t * h_tile, h_tile), h_tile)
            g = jnp.zeros((n_y * rows, h_tile), F32)
            u = jnp.zeros((n_y * rows, h_tile), F32)
            for q in range(pieces):
                block = G[pair[k], q].reshape(n_y * rows, width)
                g += jnp.dot(block, WG[q * width:(q + 1) * width, cols], preferred_element_type=F32)
            for q in range(pieces):
                block = G[pair[k], q].reshape(n_y * rows, width)
                u += jnp.dot(block, WU[q * width:(q + 1) * width, cols], preferred_element_type=F32)
            H[k, :, cols] = (g / (1.0 + jnp.exp(-g)) * u * scale).astype(BF16)
            return carry

        lax.fori_loop(0, WG.shape[1] // h_tile, tile, 0)

    def down(k):
        def tile(q, carry):
            cols = pl.ds(pl.multiple_of(q * width, width), width)
            part = jnp.dot(H[k], WD[:, cols], preferred_element_type=F32).astype(BF16)
            Y[pair[k], q] = part.reshape(n_y, rows, width)
            return carry

        lax.fori_loop(0, pieces, tile, 0)
        return send(Y.at[pair[k], other_c], RC.at[k], core_peer)

    def add(r, q, value):
        Y[r, q] = (Y[r, q].astype(F32) + value.astype(F32)).astype(BF16)

    def reduce_1(k, r0):
        got(r0)
        for j in range(n_y):
            def tile(q, carry):
                add(plane[k] * n_y + j, c * half + q, RC[k, j, q])
                return carry
            lax.fori_loop(0, half, tile, 0)
        to_y = [send(Y.at[other[k], piece(h, 0)], RY0.at[k, h], y_peer) for h in range(2)]
        to_x = send(Y.at[pair[k], piece(xo, 1)], RX1.at[k], x_peer)
        return to_y, to_x

    def reduce_2(k, r1):
        to_y, to_x = r1
        got(*to_y)
        for h in range(2):
            add(rank[k], piece(h, 0), RY0[k, h])
        x0 = send(Y.at[rank[k], piece(xo, 0)], RX0.at[k], x_peer)
        got(to_x)
        for j in range(n_y):
            add(plane[k] * n_y + j, piece(x, 1), RX1[k, j])
        y1 = send(Y.at[other[k], piece(x, 1)], RY1.at[k], y_peer)
        return x0, y1

    def reduce_3(k, r2):
        got(r2[0])
        add(rank[k], piece(x, 0), RX0[k])
        got(r2[1])
        add(rank[k], piece(x, 1), RY1[k])
        if k:
            return send(Y.at[rank[k], mine_x], RZ.at[k - 1], z_peer[k])

    got(A0)
    ref = G.at[other[0], mine_x]
    B0 = send(ref, ref, x_peer)
    A1 = stage_a(1)
    got(B0)
    ref = G.at[other[0], mine_c]
    D0 = send(ref, ref, core_peer)
    B1 = stage_b(1, A1)
    got(D0)
    got(*metas)
    weight_loads[0].wait()
    weight_loads[1].wait()
    gate_up(0)
    A2 = stage_a(2)
    B2 = stage_b(2, A2)
    D1 = stage_d(1, B1)
    A3 = stage_a(3)
    got(D1)
    gate_up(1)
    B3 = stage_b(3, A3)
    D2 = stage_d(2, B2)
    weight_loads[2].wait()
    C1 = down(1)
    got(D2)
    gate_up(2)
    D3 = stage_d(3, B3)
    P1 = reduce_1(1, C1)
    C2 = down(2)
    got(D3)
    gate_up(3)
    P2 = reduce_1(2, C2)
    Q1 = reduce_2(1, P1)
    C3 = down(3)
    C0 = down(0)
    P3 = reduce_1(3, C3)
    F1 = reduce_3(1, Q1)
    Q2 = reduce_2(2, P2)
    P0 = reduce_1(0, C0)
    F2 = reduce_3(2, Q2)
    Q3 = reduce_2(3, P3)
    F3 = reduce_3(3, Q3)
    Q0 = reduce_2(0, P0)
    reduce_3(0, Q0)

    total = M[0]
    for r in range(1, n_dp):
        total = total + M[r]
    meta_out[...] = total

    got(F1, F2, F3)
    to_x = []
    for o in range(quarter):
        value = Y[me, piece(x, o)].astype(F32)
        for k in range(n_planes - 1):
            value = value + RZ[k, o].astype(F32)
        OUT[piece(x, o)] = value.astype(BF16)
        ref = OUT.at[piece(x, o)]
        to_x.append((send(ref, ref, x_peer), send(ref, ref, core_peer)))
    stores = []

    def store(q):
        stores.append(local(OUT.at[q], out.at[:, pl.ds(pl.multiple_of(q * width, width), width)]))

    last = []
    for o in range(quarter):
        store(piece(x, o))
        got(to_x[o][0])
        ref = OUT.at[piece(xo, o)]
        last.append(send(ref, ref, core_peer))
        store(piece(xo, o))
    for o in range(quarter):
        got(to_x[o][1])
        store(co * half + x * quarter + o)
    for o in range(quarter):
        got(last[o])
        store(co * half + xo * quarter + o)
    for copy in stores:
        copy.wait()
    for copy in sent:
        copy.wait_send()


def planned(n_y, n_planes, tokens, expert_ids, gate_weights, live_counts, w_gate, w_up, w_down):
    n_experts = lax.axis_size("expert")
    rows, model = tokens.shape
    hidden = w_gate.shape[2]
    n_dp, pieces = n_y * n_planes, 8
    width, half, quarter = model // pieces, pieces // 2, pieces // 4
    weight, loads = routing_weights(
        expert_ids, gate_weights, live_counts[0], n_experts, lax.axis_index("expert")
    )
    line = jnp.zeros((rows,), F32).at[:n_experts].set(loads.astype(F32))
    meta = jnp.concatenate([weight[None], line[None], jnp.zeros((6, rows), F32)], axis=0)
    hbm = pl.BlockSpec(memory_space=pl.ANY)
    vmem = pl.BlockSpec(memory_space=pltpu.VMEM)
    mixed, totals = pl.pallas_call(
        functools.partial(kernel, n_y, n_planes),
        name="moe",
        out_shape=(jax.ShapeDtypeStruct((rows, model), BF16), jax.ShapeDtypeStruct((8, rows), F32)),
        in_specs=[hbm] * 5,
        out_specs=(hbm, vmem),
        scratch_shapes=[
            pltpu.VMEM((n_dp, pieces, rows, width), BF16),
            pltpu.VMEM((n_dp, 8, rows), F32),
            pltpu.VMEM((model, hidden), BF16),
            pltpu.VMEM((model, hidden), BF16),
            pltpu.VMEM((hidden, model), BF16),
            pltpu.VMEM((n_planes, n_y * rows, hidden), BF16),
            pltpu.VMEM((n_dp, pieces, rows, width), BF16),
            pltpu.VMEM((n_planes, n_y, half, rows, width), BF16),
            pltpu.VMEM((n_planes, 2, rows, width), BF16),
            pltpu.VMEM((n_planes, rows, width), BF16),
            pltpu.VMEM((n_planes, n_y, rows, width), BF16),
            pltpu.VMEM((n_planes, rows, width), BF16),
            pltpu.VMEM((n_planes - 1, quarter, rows, width), BF16),
            pltpu.VMEM((pieces, rows, width), BF16),
            pltpu.SemaphoreType.DMA((96,)),
            pltpu.SemaphoreType.DMA((96,)),
            pltpu.SemaphoreType.DMA((32,)),
        ],
        compiler_params=pltpu.CompilerParams(
            collective_id=0, has_side_effects=True, vmem_limit_bytes=63 * 2**20
        ),
    )(tokens, meta, w_gate, w_up, w_down)
    return mixed, totals[1, :n_experts].astype(jnp.int32)


def solution(mesh):
    n_dp, n_experts = mesh.shape["dp"], mesh.shape["expert"]
    n_x = n_experts // 2
    n_y = n_x
    n_planes = n_dp // n_y
    body = general
    if n_y == 2 and n_planes == 4:
        body = functools.partial(planned, n_y, n_planes)
    placed = (
        P("dp", None),
        P("dp", None),
        P("dp", None),
        P("dp"),
        P("expert", None, "dp"),
        P("expert", None, "dp"),
        P("expert", "dp", None),
    )
    return jax.shard_map(
        body, mesh=mesh, in_specs=placed, out_specs=(P("dp", None), P()), check_vma=False
    )
```

profile of v0, /device:TPU:9, one launch (start us, length us, event | category | flops | bytes accessed | tf_op | source)
XLA Modules:
  0.0 125.4 jit_solution(13861653436789254553)
XLA Ops:
  1.3 0.7 fusion.3
  2.0 0.8 convert_reduce_fusion
  2.8 0.1 pad.5.clone
  2.9 0.7 fusion.meta
  3.6 118.4 %moe.1 = (bf16[128,4096]{1,0:T(8,128)(2,1)}, f32[8,128]{1,0:T(8,128)}) custom-call(bf16[128,4096]{1,0:T(8,128)(2,1)} %tokens.1, f32[8,128]{1,0:T(8,128)} %fusion.meta, bf16[1,4096,1024]{2,1,0:T(8,128)(2,1)} %w_gate.1, bf16[1,4096,1024]{2,1,0:T(8,128)(2,1)} %w_up.1, bf16[1,1024,4096]{2,1,0:T(8,128)(2,1)} %w_down.1), custom_call_target="tpu_custom_call" | custom-call | tf_op jit(solution)/shard_map/moe/pallas_call | solution.py:288
  122.0 1.2 convert_bitcast_fusion
  123.1 2.3 %copy.12 = bf16[128,4096]{1,0:T(8,128)(2,1)} copy(bf16[128,4096]{1,0:T(8,128)(2,1)} %get-tuple-element.20) | data formatting | bytes 2097152
  (3 shorter events, 0.0 us)
where the time goes:
time: 127 us; the launch traced here: 125 us
  Pallas kernels  118 us (93%)
  other arithmetic  3.38 us (3%)
  local copies, waits for them, and re-layouts  2.36 us (2%)
  between operations  1.3 us (1%)
    pallas_call x1, Pallas kernels, planned(): pl.pallas_call(functools.partial(kernel, n_y, n_planes), name='moe', out_...  118 us

commit v1 on v0

v1 whole, which is shorter than its diff:
```python
import functools

import jax
import jax.numpy as jnp
from jax import lax
from jax.experimental import pallas as pl
from jax.experimental.pallas import tpu as pltpu
from jax.sharding import PartitionSpec as P

MESH = pl.DeviceIdType.MESH
BF16, F32 = jnp.bfloat16, jnp.float32


def routing_weights(expert_ids, gate_weights, live_total, n_experts, my_expert):
    live = (jnp.arange(expert_ids.shape[0], dtype=jnp.int32) < live_total)[:, None]
    mine = (expert_ids == my_expert) & live
    weight = jnp.sum(jnp.where(mine, gate_weights, 0.0), axis=1)
    named = (expert_ids[:, :, None] == jnp.arange(n_experts, dtype=jnp.int32)) & live[:, :, None]
    return weight, jnp.sum(named.astype(jnp.int32), axis=(0, 1))


def general(tokens, expert_ids, gate_weights, live_counts, w_gate, w_up, w_down):
    weight, loads = routing_weights(
        expert_ids, gate_weights, live_counts[0], lax.axis_size("expert"), lax.axis_index("expert")
    )
    rows = lax.all_gather(tokens, "dp", axis=0, tiled=True)
    scale = lax.all_gather(weight, "dp", axis=0, tiled=True)[:, None]
    gate_act = jnp.dot(rows, w_gate[0], preferred_element_type=F32)
    up_act = jnp.dot(rows, w_up[0], preferred_element_type=F32)
    hidden = (jax.nn.silu(gate_act) * up_act * scale).astype(BF16)
    partial = jnp.dot(hidden, w_down[0], preferred_element_type=F32).astype(BF16)
    summed = lax.psum_scatter(partial, "dp", scatter_dimension=0, tiled=True)
    return lax.psum(summed, "expert"), lax.psum(loads, "dp")


def kernel(n_y, n_planes, n_experts, tokens, ids, gates, live, w_gate, w_up, w_down, out, totals,
           G, M, IDS, GATES, WG, WU, WD, H, Y, RC, RT, RS, RZ1, RL, RZ, OUT, send_sem, recv_sem, local_sem):
    dp, ex = lax.axis_index("dp"), lax.axis_index("expert")
    z, y = dp // n_y, dp % n_y
    x, c = ex // 2, ex % 2
    yo, xo, co = 1 - y, 1 - x, 1 - c
    n_dp = n_y * n_planes
    pieces, rows, width = G.shape[1:]
    half, quarter = pieces // 2, pieces // 4
    both, far = range(2), range(2, n_planes)

    low = z < n_planes // 2
    mid = (z > 0) & (z < n_planes - 1)
    near, beyond = jnp.where(low, 2, 1), jnp.where(low, n_planes - 1, 0)
    plane = [z, z + 1 - 2 * (z % 2), near, beyond]
    kind = jnp.where(mid, 0, 1)
    y_peer, x_peer, core_peer = (z * n_y + yo, ex), (dp, xo * 2 + c), (dp, x * 2 + co)
    z_peer = [(plane[k] * n_y + y, ex) for k in range(n_planes)]
    me = dp
    rank = [plane[k] * n_y + y for k in range(n_planes)]
    other = [plane[k] * n_y + yo for k in range(n_planes)]
    pair = [pl.ds(plane[k] * n_y, n_y) for k in range(n_planes)]
    member = [[plane[k] * n_y + j for j in range(n_y)] for k in range(n_planes)]
    dp_peers = [(lax.rem(dp + d, n_dp), ex) for d in range(1, n_dp)]
    peers = dp_peers + [x_peer, core_peer]
    barrier = pltpu.get_barrier_semaphore()

    n_local = [0]

    def local(src, dst):
        copy = pltpu.make_async_copy(src, dst, local_sem.at[n_local[0]])
        n_local[0] += 1
        copy.start()
        return copy

    route_loads = [local(ids, IDS), local(gates, GATES)]
    own_loads = [local(tokens.at[:, pl.ds(q * width, width)], G.at[me, q]) for q in range(pieces)]

    for a, b in peers:
        pl.semaphore_signal(barrier, inc=1, device_id={"dp": a, "expert": b}, device_id_type=MESH)

    weight_loads = [local(w_gate.at[0], WG), local(w_up.at[0], WU), local(w_down.at[0], WD)]

    sent = []

    def link(src, dst, to, slot=None):
        i = len(sent)
        copy = pltpu.make_async_remote_copy(
            src_ref=src, dst_ref=dst, send_sem=send_sem.at[i], recv_sem=recv_sem.at[i if slot is None else slot],
            device_id={"dp": to[0], "expert": to[1]}, device_id_type=MESH,
        )
        sent.append(copy)
        return copy

    def same(ref, to):
        return link(ref, ref, to)

    def arrival(ref, slot):
        return pltpu.make_async_remote_copy(
            src_ref=ref, dst_ref=ref, send_sem=send_sem.at[slot], recv_sem=recv_sem.at[slot],
            device_id={"dp": dp, "expert": ex}, device_id_type=MESH,
        )

    def go(*copies):
        for copy in copies:
            copy.start()

    def got(*copies):
        for copy in copies:
            copy.wait_recv()

    mine_c, other_c = pl.ds(c * half, half), pl.ds(co * half, half)
    P = [[c * half + h * quarter + o for o in range(quarter)] for h in range(2)]
    mx = [c * half + x * quarter + o for o in range(quarter)]
    ox = [c * half + xo * quarter + o for o in range(quarter)]

    metas = [same(M.at[me], peer) for peer in dp_peers]
    A0 = [same(G.at[me, mx[o]], y_peer) for o in both]
    B0 = [same(G.at[other[0], mx[o]], x_peer) for o in both]
    D0 = [same(G.at[other[0], mx[o]], core_peer) for o in both] + [same(G.at[other[0], ox[o]], core_peer) for o in both]

    def halves(k, o, by_y):
        if by_y:
            return [(rank[k], P[i][o]) for i in both]
        return [(member[k][i], mx[o]) for i in both]

    def hop(by_y):
        return y_peer if by_y else x_peer

    y_first = [None, (True, False), (False, True), (True, False)]
    Z1 = [[same(G.at[r, q], z_peer[1]) for r, q in halves(0, o, y_first[1][o])] for o in both]
    F1 = [[same(G.at[r, q], hop(y_first[1][o])) for r, q in halves(1, o, y_first[1][o])] for o in both]
    D1 = [
        [same(G.at[r, q], core_peer) for r, q in halves(1, o, y_first[1][o])]
        + [same(G.at[other[1], P[i][o]] if y_first[1][o] else G.at[member[1][i], ox[o]], core_peer) for i in both]
        for o in both
    ]
    ZS, GX, GY, GH, DZ, DF, DR = [[None, None] for _ in range(7)]
    first = len(sent)
    for k in far:
        ZS.append([link(G.at[me, mx[o]], G.at[me, mx[o]], z_peer[k], first + kind * 2 + o) for o in both])
    for k in far:
        near_x = [(other[k], mx[o]) if y_first[k][o] else (rank[k], ox[o]) for o in both]
        last_x = [(rank[k], ox[o]) if y_first[k][o] else (other[k], mx[o]) for o in both]
        GX.append([same(G.at[rank[k], mx[o]], x_peer) for o in both])
        GY.append([same(G.at[rank[k], mx[o]], y_peer) for o in both])
        GH.append([same(G.at[near_x[o]], x_peer if y_first[k][o] else y_peer) for o in both])
        DZ.append([same(G.at[rank[k], mx[o]], core_peer) for o in both])
        DF.append([same(G.at[near_x[o]], core_peer) for o in both])
        DR.append([[same(G.at[last_x[o]], core_peer), same(G.at[other[k], ox[o]], core_peer)] for o in both])
    ZG = [None, None] + [[arrival(G.at[me, mx[o]], first + (k - 2) * 2 + o) for o in both] for k in far]

    sum_y = [(True, False), (True, False), (False, True), (False, True)]
    C = [link(Y.at[pair[k], other_c], RC.at[k], core_peer) for k in range(n_planes)]
    T, TG, S = [], [], [None, None]
    for k in range(n_planes):
        T.append([
            [
                link(Y.at[other[k], P[i][o]], RT.at[k, o, i], y_peer)
                if sum_y[k][o]
                else link(Y.at[member[k][i], ox[o]], RT.at[k, o, i], x_peer)
                for i in both
            ]
            for o in both
        ])
        TG.append([halves(k, o, sum_y[k][o]) for o in both])
    for k in far:
        S.append([
            link(Y.at[rank[k], ox[o]], RS.at[k - 2, o], x_peer)
            if sum_y[k][o]
            else link(Y.at[other[k], mx[o]], RS.at[k - 2, o], y_peer)
            for o in both
        ])
    start = len(sent)
    ZR = [None, None] + [
        [link(Y.at[rank[k], mx[o]], RZ.at[kind, o], z_peer[k], start + kind * 2 + o) for o in both] for k in far
    ]
    ZA = [[arrival(RZ.at[i, o], start + i * 2 + o) for o in both] for i in both]
    ZR1 = [[link(Y.at[TG[1][o][i]], RZ1.at[o, i], z_peer[1]) for i in both] for o in both]
    L0 = [
        link(Y.at[me, ox[o]], RL.at[o], x_peer) if sum_y[0][o] else link(Y.at[other[0], mx[o]], RL.at[o], y_peer)
        for o in both
    ]
    FX = [same(OUT.at[mx[o]], x_peer) for o in both]
    FC = [same(OUT.at[mx[o]], core_peer) for o in both]
    LC = [same(OUT.at[ox[o]], core_peer) for o in both]

    for copy in route_loads:
        copy.wait()
    lane = lax.broadcasted_iota(jnp.int32, IDS.shape, 1)
    alive = lane < live[0]
    named = IDS[...]
    weight = jnp.sum(jnp.where((named == ex) & alive, GATES[...], 0.0), axis=0, keepdims=True)
    row = lax.broadcasted_iota(jnp.int32, M.shape[1:], 0)
    col = lax.broadcasted_iota(jnp.int32, M.shape[1:], 1)
    line = jnp.where(row == 0, weight, 0.0)
    for e in range(n_experts):
        count = jnp.sum(jnp.where((named == e) & alive, 1.0, 0.0))
        line = jnp.where((row == 1) & (col == e), count, line)
    M[me] = line

    for copy in own_loads:
        copy.wait()
    pl.semaphore_wait(barrier, len(peers))

    go(*metas)
    first_sends = [copy for o in both for copy in (A0[o], ZS[3][o], ZS[2][o])] + Z1[0]

    def st(i):
        go(first_sends[i])

    h_tile = min(256, WG.shape[1])

    def a0(o):
        got(A0[o])
        go(B0[o], D0[o])
        if o:
            go(*Z1[1])

    def b0(o):
        got(B0[o])
        go(D0[2 + o])

    def fz(o, i):
        got(Z1[o][i])
        go(F1[o][i], D1[o][i])

    def zg(k, o):
        got(ZG[k][o])
        go(*((GY[k][o], GX[k][o]) if y_first[k][o] else (GX[k][o], GY[k][o])), DZ[k][o])

    def gh(k, o):
        got((GX, GY)[y_first[k][o]][k][o])
        go(GH[k][o], DF[k][o])

    def f1(o, i):
        got(F1[o][i])
        go(D1[o][2 + i])

    def gb(k, o):
        got((GY, GX)[y_first[k][o]][k][o])
        go(DR[k][o][0])

    def gc(k, o):
        got(GH[k][o])
        go(DR[k][o][1])

    def whole(k):
        if k == 0:
            got(*D0)
        elif k == 1:
            got(*D1[0], *D1[1])
        else:
            got(*DZ[k], *DF[k], *DR[k][0], *DR[k][1])

    def tiles(tile, lo, hi):
        if hi - lo == 1:
            tile(lo)
        else:
            lax.fori_loop(lo, hi, lambda i, carry: (tile(i), carry)[1], 0, unroll=True)

    scales = {}

    def gate_up(k, lo, hi):
        if k not in scales:
            if not scales:
                got(*metas)
                weight_loads[0].wait()
                weight_loads[1].wait()
            columns = [jnp.transpose(M[member[k][j]])[:, 0:1] for j in range(n_y)]
            scales[k] = jnp.concatenate(columns, axis=0)

        def tile(t):
            cols = pl.ds(t * h_tile if isinstance(t, int) else pl.multiple_of(t * h_tile, h_tile), h_tile)
            lhs = jnp.concatenate([G[pair[k], q].reshape(n_y * rows, width) for q in range(pieces)], axis=1)
            g = jnp.dot(lhs, WG[:, cols], preferred_element_type=F32)
            u = jnp.dot(lhs, WU[:, cols], preferred_element_type=F32)
            H[k, :, cols] = (g / (1.0 + jnp.exp(-g)) * u * scales[k]).astype(BF16)

        tiles(tile, lo, hi)

    downs = []

    def down(k, lo, hi):
        if not downs:
            weight_loads[2].wait()
        downs.append(k)

        def tile(t):
            q = lax.rem(co * half + 2 * t, pieces)
            cols = pl.ds(pl.multiple_of(q * width, width), 2 * width)
            part = jnp.dot(H[k], WD[:, cols], preferred_element_type=F32).astype(BF16)
            for i in range(2):
                Y[pair[k], q + i] = part[:, i * width:(i + 1) * width].reshape(n_y, rows, width)

        tiles(tile, lo, hi)

    def add(r, q, value):
        Y[r, q] = (Y[r, q].astype(F32) + value.astype(F32)).astype(BF16)

    def r1(k):
        got(C[k])
        for j in range(n_y):
            def tile(q, carry):
                add(member[k][j], c * half + q, RC[k, j, q])
                return carry
            lax.fori_loop(0, half, tile, 0)
        go(T[k][0][0], T[k][1][0], T[k][0][1], T[k][1][1])

    def r2(k, o):
        for i in both:
            got(T[k][o][i])
            add(*TG[k][o][i], RT[k, o, i])
            if k == 1:
                go(ZR1[o][i])
        if k > 1:
            go(S[k][o])

    def r3(k, o):
        got(S[k][o])
        add(rank[k], mx[o], RS[k - 2, o])
        go(ZR[k][o])

    def rz1(o):
        for i in both:
            got(ZR1[o][i])
            add(*TG[0][o][i], RZ1[o, i])
        go(L0[o])

    def last(o):
        got(L0[o])
        total = Y[me, mx[o]].astype(F32) + RL[o].astype(F32)
        got(ZA[0][o], ZA[1][o])
        OUT[mx[o]] = (total + RZ[0, o].astype(F32) + RZ[1, o].astype(F32)).astype(BF16)
        go(FX[o], FC[o])
        store(mx[o])

    stores = []

    def store(q):
        stores.append(local(OUT.at[q], out.at[:, pl.ds(pl.multiple_of(q * width, width), width)]))

    def fin(o):
        got(FX[o])
        go(LC[o])
        store(ox[o])

    def loads():
        count = M[0]
        for r in range(1, n_dp):
            count = count + M[r]
        for e in range(n_experts):
            totals[e] = jnp.sum(jnp.where((row == 1) & (col == e), count, 0.0)).astype(jnp.int32)

    st(5)
    st(4)
    st(2)
    st(1)
    st(3)
    st(0)
    a0(1)
    a0(0)
    st(6)
    zg(3, 1)
    zg(3, 0)
    b0(1)
    gb(3, 1)
    b0(0)
    whole(0)
    gate_up(0, 0, 1)
    gh(3, 1)
    gh(3, 0)
    gate_up(0, 1, 2)
    st(7)
    gate_up(0, 2, 3)
    fz(1, 0)
    gate_up(0, 3, 4)
    zg(2, 1)
    gb(3, 0)
    gc(3, 0)
    gc(3, 1)
    whole(3)
    gate_up(3, 0, 1)
    fz(0, 0)
    fz(1, 1)
    gate_up(3, 1, 3)
    fz(0, 1)
    gh(2, 1)
    zg(2, 0)
    gate_up(3, 3, 4)
    down(3, 0, 2)
    go(C[3])
    down(3, 2, 4)
    r1(3)
    f1(0, 1)
    f1(1, 1)
    f1(0, 0)
    f1(1, 0)
    down(0, 0, 2)
    go(C[0])
    gb(2, 0)
    down(0, 2, 4)
    whole(1)
    gate_up(1, 0, 2)
    gc(2, 1)
    gh(2, 0)
    gb(2, 1)
    gate_up(1, 2, 3)
    r2(3, 1)
    gate_up(1, 3, 4)
    r2(3, 0)
    down(1, 0, 1)
    r1(0)
    down(1, 1, 2)
    go(C[1])
    down(1, 2, 4)
    gc(2, 0)
    r3(3, 1)
    r1(1)
    whole(2)
    gate_up(2, 0, 4)
    r3(3, 0)
    down(2, 0, 2)
    go(C[2])
    down(2, 2, 4)
    r2(1, 1)
    r1(2)
    r2(1, 0)
    r2(0, 1)
    r2(2, 1)
    r2(2, 0)
    r2(0, 0)
    r3(2, 1)
    r3(2, 0)
    rz1(1)
    rz1(0)
    loads()
    last(1)
    last(0)
    fin(1)
    fin(0)

    for o in both:
        got(FC[o])
        store(co * half + x * quarter + o)
    for o in both:
        got(LC[o])
        store(co * half + xo * quarter + o)
    for copy in stores:
        copy.wait()
    for copy in sent:
        copy.wait_send()


def planned(n_y, n_planes, tokens, expert_ids, gate_weights, live_counts, w_gate, w_up, w_down):
    n_experts = lax.axis_size("expert")
    rows, model = tokens.shape
    hidden = w_gate.shape[2]
    n_dp, pieces = n_y * n_planes, 8
    width, half, quarter = model // pieces, pieces // 2, pieces // 4
    hbm = pl.BlockSpec(memory_space=pl.ANY)
    smem = pl.BlockSpec(memory_space=pltpu.SMEM)
    return pl.pallas_call(
        functools.partial(kernel, n_y, n_planes, n_experts),
        name="moe",
        out_shape=(jax.ShapeDtypeStruct((rows, model), BF16), jax.ShapeDtypeStruct((n_experts,), jnp.int32)),
        in_specs=[hbm] * 3 + [smem] + [hbm] * 3,
        out_specs=(hbm, smem),
        scratch_shapes=[
            pltpu.VMEM((n_dp, pieces, rows, width), BF16),
            pltpu.VMEM((n_dp, 8, rows), F32),
            pltpu.VMEM((2, rows), jnp.int32),
            pltpu.VMEM((2, rows), F32),
            pltpu.VMEM((model, hidden), BF16),
            pltpu.VMEM((model, hidden), BF16),
            pltpu.VMEM((hidden, model), BF16),
            pltpu.VMEM((n_planes, n_y * rows, hidden), BF16),
            pltpu.VMEM((n_dp, pieces, rows, width), BF16),
            pltpu.VMEM((n_planes, n_y, half, rows, width), BF16),
            pltpu.VMEM((n_planes, 2, 2, rows, width), BF16),
            pltpu.VMEM((2, 2, rows, width), BF16),
            pltpu.VMEM((2, 2, rows, width), BF16),
            pltpu.VMEM((2, rows, width), BF16),
            pltpu.VMEM((2, 2, rows, width), BF16),
            pltpu.VMEM((pieces, rows, width), BF16),
            pltpu.SemaphoreType.DMA((128,)),
            pltpu.SemaphoreType.DMA((128,)),
            pltpu.SemaphoreType.DMA((32,)),
        ],
        compiler_params=pltpu.CompilerParams(
            collective_id=0, has_side_effects=True, vmem_limit_bytes=63 * 2**20
        ),
    )(tokens, expert_ids.T, gate_weights.T, live_counts, w_gate, w_up, w_down)


def solution(mesh):
    n_dp, n_experts = mesh.shape["dp"], mesh.shape["expert"]
    n_x = n_experts // 2
    n_y = n_x
    n_planes = n_dp // n_y
    body = general
    if n_y == 2 and n_planes == 4:
        body = functools.partial(planned, n_y, n_planes)
    placed = (
        P("dp", None),
        P("dp", None),
        P("dp", None),
        P("dp"),
        P("expert", None, "dp"),
        P("expert", None, "dp"),
        P("expert", "dp", None),
    )
    return jax.shard_map(
        body, mesh=mesh, in_specs=placed, out_specs=(P("dp", None), P()), check_vma=False
    )
```

time: 127 us -> 96.4 us (0.76); the launches traced: 125 us -> 96.2 us
  Pallas kernels: 118 us -> 91.5 us
  other arithmetic: 3.38 us -> 0 us
    pallas_call x1, Pallas kernels: 118 us -> 91.5 us  [planned(): pl.pallas_call(functools.partial(kernel, n_y, n_planes, n_experts), name=...]
    reduce_sum x2 -> x0, other arithmetic: 1.51 us -> none  [the longest x1 0.8 us: routing_weights(): return (weight, jnp.sum(named.astype(jnp.int32), axis=(0, 1)))]
    unnamed x1 -> x2, local copies, waits for them, and re-layouts: 2.29 us -> 3.4 us
where the time goes in v1:
time: 96.4 us; the launch traced here: 96.2 us
  Pallas kernels  91.5 us (95%)
  local copies, waits for them, and re-layouts  3.4 us (4%)
  between operations  1.29 us (1%)
    pallas_call x1, Pallas kernels, planned(): pl.pallas_call(functools.partial(kernel, n_y, n_planes, n_experts), name=...  91.5 us
    unnamed x2, local copies, waits for them, and re-layouts  3.4 us

profile of v1, /device:TPU:9, one launch (start us, length us, event | category | flops | bytes accessed | tf_op | source)
XLA Modules:
  0.0 96.2 jit_solution(4519478247965401109)
XLA Ops:
  1.3 91.5 %moe.1 = (bf16[128,4096]{1,0:T(8,128)(2,1)}, s32[4]{0:T(128)}) custom-call(bf16[128,4096]{1,0:T(8,128)(2,1)} %tokens.1, s32[2,128]{1,0:T(2,128)} %bitcast.2, f32[2,128]{1,0:T(2,128)} %bitcast.3, s32[1]{0:T(128)S(6)} %copy.11.live, bf16[1,4096,1024]{2,1,0:T(8,128)(2,1)} %w_gate.1, bf16[1,4096,1024]{2,1,0:T(8,128)(2,1)} %w_up.1, bf16[1,1024,4096]{2,1,0:T(8,128)(2,1)} %w_down.1), custom_call_target="tpu_custom_call" | custom-call | tf_op jit(solution)/shard_map/moe/pallas_call | solution.py:458
  92.8 2.3 %copy.12 = bf16[128,4096]{1,0:T(8,128)(2,1)} copy(bf16[128,4096]{1,0:T(8,128)(2,1)} %get-tuple-element.4) | data formatting | bytes 2097152
  95.1 1.1 %copy.13 = s32[4]{0:T(128)} copy(s32[4]{0:T(128)} %get-tuple-element.5) | data formatting | bytes 32

commit v2 on v1

--- a/solution.py
+++ b/solution.py
@@ -33,8 +33,8 @@
     return lax.psum(summed, "expert"), lax.psum(loads, "dp")
 
 
-def kernel(n_y, n_planes, n_experts, tokens, ids, gates, live, w_gate, w_up, w_down, out, totals,
-           G, M, IDS, GATES, WG, WU, WD, H, Y, RC, RT, RS, RZ1, RL, RZ, OUT, send_sem, recv_sem, local_sem):
+def kernel(n_y, n_planes, n_experts, tokens, ids, gates, live, w_gate, w_up, w_down, OUT, LOADS,
+           G, M, IDS, GATES, WG, WU, WD, H, Y, RC, RT, RS, RZ1, RL, RZ, send_sem, recv_sem, local_sem):
     dp, ex = lax.axis_index("dp"), lax.axis_index("expert")
     z, y = dp // n_y, dp % n_y
     x, c = ex // 2, ex % 2
@@ -42,7 +42,7 @@
     n_dp = n_y * n_planes
     pieces, rows, width = G.shape[1:]
     half, quarter = pieces // 2, pieces // 4
-    both, far = range(2), range(2, n_planes)
+    both, far, parts = range(2), range(2, n_planes), range(quarter)
 
     low = z < n_planes // 2
     mid = (z > 0) & (z < n_planes - 1)
@@ -110,9 +110,9 @@
     ox = [c * half + xo * quarter + o for o in range(quarter)]
 
     metas = [same(M.at[me], peer) for peer in dp_peers]
-    A0 = [same(G.at[me, mx[o]], y_peer) for o in both]
-    B0 = [same(G.at[other[0], mx[o]], x_peer) for o in both]
-    D0 = [same(G.at[other[0], mx[o]], core_peer) for o in both] + [same(G.at[other[0], ox[o]], core_peer) for o in both]
+    A0 = [same(G.at[me, mx[o]], y_peer) for o in parts]
+    B0 = [same(G.at[other[0], mx[o]], x_peer) for o in parts]
+    D0 = [[same(G.at[other[0], q[o]], core_peer) for o in parts] for q in (mx, ox)]
 
     def halves(k, o, by_y):
         if by_y:
@@ -122,30 +122,30 @@
     def hop(by_y):
         return y_peer if by_y else x_peer
 
-    y_first = [None, (True, False), (False, True), (True, False)]
-    Z1 = [[same(G.at[r, q], z_peer[1]) for r, q in halves(0, o, y_first[1][o])] for o in both]
-    F1 = [[same(G.at[r, q], hop(y_first[1][o])) for r, q in halves(1, o, y_first[1][o])] for o in both]
+    y_first = [None, (False, False, True, True), (False, False, True, True), (True, True, False, False)]
+    Z1 = [[same(G.at[r, q], z_peer[1]) for r, q in halves(0, o, y_first[1][o])] for o in parts]
+    F1 = [[same(G.at[r, q], hop(y_first[1][o])) for r, q in halves(1, o, y_first[1][o])] for o in parts]
     D1 = [
         [same(G.at[r, q], core_peer) for r, q in halves(1, o, y_first[1][o])]
         + [same(G.at[other[1], P[i][o]] if y_first[1][o] else G.at[member[1][i], ox[o]], core_peer) for i in both]
-        for o in both
+        for o in parts
     ]
     ZS, GX, GY, GH, DZ, DF, DR = [[None, None] for _ in range(7)]
     first = len(sent)
     for k in far:
-        ZS.append([link(G.at[me, mx[o]], G.at[me, mx[o]], z_peer[k], first + kind * 2 + o) for o in both])
+        ZS.append([link(G.at[me, mx[o]], G.at[me, mx[o]], z_peer[k], first + kind * quarter + o) for o in parts])
     for k in far:
-        near_x = [(other[k], mx[o]) if y_first[k][o] else (rank[k], ox[o]) for o in both]
-        last_x = [(rank[k], ox[o]) if y_first[k][o] else (other[k], mx[o]) for o in both]
-        GX.append([same(G.at[rank[k], mx[o]], x_peer) for o in both])
-        GY.append([same(G.at[rank[k], mx[o]], y_peer) for o in both])
-        GH.append([same(G.at[near_x[o]], x_peer if y_first[k][o] else y_peer) for o in both])
-        DZ.append([same(G.at[rank[k], mx[o]], core_peer) for o in both])
-        DF.append([same(G.at[near_x[o]], core_peer) for o in both])
-        DR.append([[same(G.at[last_x[o]], core_peer), same(G.at[other[k], ox[o]], core_peer)] for o in both])
-    ZG = [None, None] + [[arrival(G.at[me, mx[o]], first + (k - 2) * 2 + o) for o in both] for k in far]
-
-    sum_y = [(True, False), (True, False), (False, True), (False, True)]
+        near_x = [(other[k], mx[o]) if y_first[k][o] else (rank[k], ox[o]) for o in parts]
+        last_x = [(rank[k], ox[o]) if y_first[k][o] else (other[k], mx[o]) for o in parts]
+        GX.append([same(G.at[rank[k], mx[o]], x_peer) for o in parts])
+        GY.append([same(G.at[rank[k], mx[o]], y_peer) for o in parts])
+        GH.append([same(G.at[near_x[o]], x_peer if y_first[k][o] else y_peer) for o in parts])
+        DZ.append([same(G.at[rank[k], mx[o]], core_peer) for o in parts])
+        DF.append([same(G.at[near_x[o]], core_peer) for o in parts])
+        DR.append([[same(G.at[last_x[o]], core_peer), same(G.at[other[k], ox[o]], core_peer)] for o in parts])
+    ZG = [None, None] + [[arrival(G.at[me, mx[o]], first + (k - 2) * quarter + o) for o in parts] for k in far]
+
+    sum_y = [(True, True, False, False), (True, True, False, False), (True, True, False, False), (True, True, False, False)]
     C = [link(Y.at[pair[k], other_c], RC.at[k], core_peer) for k in range(n_planes)]
     T, TG, S = [], [], [None, None]
     for k in range(n_planes):
@@ -156,29 +156,29 @@
                 else link(Y.at[member[k][i], ox[o]], RT.at[k, o, i], x_peer)
                 for i in both
             ]
-            for o in both
+            for o in parts
         ])
-        TG.append([halves(k, o, sum_y[k][o]) for o in both])
+        TG.append([halves(k, o, sum_y[k][o]) for o in parts])
     for k in far:
         S.append([
             link(Y.at[rank[k], ox[o]], RS.at[k - 2, o], x_peer)
             if sum_y[k][o]
             else link(Y.at[other[k], mx[o]], RS.at[k - 2, o], y_peer)
-            for o in both
+            for o in parts
         ])
     start = len(sent)
     ZR = [None, None] + [
-        [link(Y.at[rank[k], mx[o]], RZ.at[kind, o], z_peer[k], start + kind * 2 + o) for o in both] for k in far
+        [link(Y.at[rank[k], mx[o]], RZ.at[kind, o], z_peer[k], start + kind * quarter + o) for o in parts] for k in far
     ]
-    ZA = [[arrival(RZ.at[i, o], start + i * 2 + o) for o in both] for i in both]
-    ZR1 = [[link(Y.at[TG[1][o][i]], RZ1.at[o, i], z_peer[1]) for i in both] for o in both]
+    ZA = [[arrival(RZ.at[i, o], start + i * quarter + o) for o in parts] for i in both]
+    ZR1 = [[link(Y.at[TG[1][o][i]], RZ1.at[o, i], z_peer[1]) for i in both] for o in parts]
     L0 = [
         link(Y.at[me, ox[o]], RL.at[o], x_peer) if sum_y[0][o] else link(Y.at[other[0], mx[o]], RL.at[o], y_peer)
-        for o in both
+        for o in parts
     ]
-    FX = [same(OUT.at[mx[o]], x_peer) for o in both]
-    FC = [same(OUT.at[mx[o]], core_peer) for o in both]
-    LC = [same(OUT.at[ox[o]], core_peer) for o in both]
+    FX = [same(OUT.at[mx[o]], x_peer) for o in parts]
+    FC = [same(OUT.at[mx[o]], core_peer) for o in parts]
+    LC = [same(OUT.at[ox[o]], core_peer) for o in parts]
 
     for copy in route_loads:
         copy.wait()
@@ -199,7 +199,8 @@
     pl.semaphore_wait(barrier, len(peers))
 
     go(*metas)
-    first_sends = [copy for o in both for copy in (A0[o], ZS[3][o], ZS[2][o])] + Z1[0]
+    first_sends = [copy for o in parts for copy in (A0[o], ZS[3][o], ZS[2][o])]
+    first_sends += [copy for o in parts if y_first[1][o] for copy in Z1[o]]
 
     def st(i):
         go(first_sends[i])
@@ -208,13 +209,13 @@
 
     def a0(o):
         got(A0[o])
-        go(B0[o], D0[o])
-        if o:
-            go(*Z1[1])
+        go(B0[o], D0[0][o])
+        if not y_first[1][o]:
+            go(*Z1[o])
 
     def b0(o):
         got(B0[o])
-        go(D0[2 + o])
+        go(D0[1][o])
 
     def fz(o, i):
         got(Z1[o][i])
@@ -242,11 +243,11 @@
 
     def whole(k):
         if k == 0:
-            got(*D0)
+            got(*D0[0], *D0[1])
         elif k == 1:
-            got(*D1[0], *D1[1])
+            got(*[copy for o in parts for copy in D1[o]])
         else:
-            got(*DZ[k], *DF[k], *DR[k][0], *DR[k][1])
+            got(*DZ[k], *DF[k], *[copy for o in parts for copy in DR[k][o]])
 
     def tiles(tile, lo, hi):
         if hi - lo == 1:
@@ -274,7 +275,7 @@
 
         tiles(tile, lo, hi)
 
-    downs = []
+    downs, per = [], pieces // 4
 
     def down(k, lo, hi):
         if not downs:
@@ -282,10 +283,10 @@
         downs.append(k)
 
         def tile(t):
-            q = lax.rem(co * half + 2 * t, pieces)
-            cols = pl.ds(pl.multiple_of(q * width, width), 2 * width)
+            q = lax.rem(co * half + per * t, pieces)
+            cols = pl.ds(pl.multiple_of(q * width, width), per * width)
             part = jnp.dot(H[k], WD[:, cols], preferred_element_type=F32).astype(BF16)
-            for i in range(2):
+            for i in range(per):
                 Y[pair[k], q + i] = part[:, i * width:(i + 1) * width].reshape(n_y, rows, width)
 
         tiles(tile, lo, hi)
@@ -300,7 +301,7 @@
                 add(member[k][j], c * half + q, RC[k, j, q])
                 return carry
             lax.fori_loop(0, half, tile, 0)
-        go(T[k][0][0], T[k][1][0], T[k][0][1], T[k][1][1])
+        go(*[T[k][o][i] for i in both for o in parts])
 
     def r2(k, o):
         for i in both:
@@ -328,139 +329,200 @@
         got(ZA[0][o], ZA[1][o])
         OUT[mx[o]] = (total + RZ[0, o].astype(F32) + RZ[1, o].astype(F32)).astype(BF16)
         go(FX[o], FC[o])
-        store(mx[o])
-
-    stores = []
-
-    def store(q):
-        stores.append(local(OUT.at[q], out.at[:, pl.ds(pl.multiple_of(q * width, width), width)]))
 
     def fin(o):
         got(FX[o])
         go(LC[o])
-        store(ox[o])
 
     def loads():
         count = M[0]
         for r in range(1, n_dp):
             count = count + M[r]
-        for e in range(n_experts):
-            totals[e] = jnp.sum(jnp.where((row == 1) & (col == e), count, 0.0)).astype(jnp.int32)
-
+        LOADS[...] = count
+
+    st(9)
+    st(2)
+    st(6)
+    st(1)
+    st(0)
+    st(7)
+    st(3)
+    st(10)
+    st(8)
+    a0(3)
+    st(4)
+    st(11)
+    a0(2)
     st(5)
-    st(4)
-    st(2)
-    st(1)
-    st(3)
-    st(0)
+    zg(3, 0)
+    st(14)
+    a0(0)
     a0(1)
-    a0(0)
-    st(6)
+    zg(3, 2)
     zg(3, 1)
-    zg(3, 0)
+    b0(2)
+    b0(3)
+    gh(3, 2)
     b0(1)
-    gb(3, 1)
     b0(0)
     whole(0)
-    gate_up(0, 0, 1)
+    zg(3, 3)
+    gh(3, 0)
+    gate_up(0, 0, 2)
+    zg(2, 0)
+    gb(3, 0)
+    st(13)
+    gate_up(0, 2, 3)
+    gh(3, 3)
+    gb(3, 2)
     gh(3, 1)
-    gh(3, 0)
-    gate_up(0, 1, 2)
-    st(7)
-    gate_up(0, 2, 3)
+    gc(3, 2)
+    gate_up(0, 3, 4)
+    st(12)
+    st(15)
+    zg(2, 2)
+    down(0, 0, 1)
     fz(1, 0)
-    gate_up(0, 3, 4)
-    zg(2, 1)
-    gb(3, 0)
+    gb(3, 3)
+    fz(3, 0)
     gc(3, 0)
+    gb(3, 1)
+    gc(3, 3)
     gc(3, 1)
+    down(0, 1, 2)
+    go(C[0])
+    fz(1, 1)
+    fz(0, 0)
+    zg(2, 3)
     whole(3)
     gate_up(3, 0, 1)
-    fz(0, 0)
-    fz(1, 1)
-    gate_up(3, 1, 3)
+    fz(2, 1)
     fz(0, 1)
-    gh(2, 1)
-    zg(2, 0)
+    gate_up(3, 1, 2)
+    fz(2, 0)
+    gate_up(3, 2, 3)
+    fz(3, 1)
+    f1(1, 1)
+    gh(2, 0)
+    gh(2, 2)
     gate_up(3, 3, 4)
+    gh(2, 3)
+    f1(3, 0)
     down(3, 0, 2)
     go(C[3])
-    down(3, 2, 4)
+    zg(2, 1)
+    down(3, 2, 3)
+    f1(1, 0)
+    down(0, 2, 3)
+    f1(2, 1)
+    f1(0, 0)
+    f1(0, 1)
+    f1(2, 0)
+    down(3, 3, 4)
     r1(3)
-    f1(0, 1)
-    f1(1, 1)
-    f1(0, 0)
-    f1(1, 0)
-    down(0, 0, 2)
-    go(C[0])
+    f1(3, 1)
+    down(0, 3, 4)
+    gc(2, 2)
+    whole(1)
+    gate_up(1, 0, 1)
+    gc(2, 0)
+    gc(2, 3)
+    gh(2, 1)
+    gate_up(1, 1, 4)
+    r2(3, 0)
     gb(2, 0)
-    down(0, 2, 4)
-    whole(1)
-    gate_up(1, 0, 2)
+    r2(3, 2)
+    down(1, 0, 2)
+    go(C[1])
+    r2(3, 1)
+    gb(2, 1)
+    gb(2, 3)
+    r2(3, 3)
+    down(1, 2, 3)
+    gb(2, 2)
+    r3(3, 0)
+    r1(0)
     gc(2, 1)
-    gh(2, 0)
-    gb(2, 1)
-    gate_up(1, 2, 3)
-    r2(3, 1)
-    gate_up(1, 3, 4)
-    r2(3, 0)
-    down(1, 0, 1)
-    r1(0)
-    down(1, 1, 2)
-    go(C[1])
-    down(1, 2, 4)
-    gc(2, 0)
-    r3(3, 1)
+    down(1, 3, 4)
     r1(1)
     whole(2)
-    gate_up(2, 0, 4)
-    r3(3, 0)
+    gate_up(2, 0, 1)
+    r3(3, 1)
+    gate_up(2, 1, 3)
+    r3(3, 2)
+    gate_up(2, 3, 4)
     down(2, 0, 2)
     go(C[2])
-    down(2, 2, 4)
+    r2(0, 0)
+    down(2, 2, 3)
+    r2(1, 2)
+    down(2, 3, 4)
+    r1(2)
+    r3(3, 3)
+    r2(1, 0)
+    r2(1, 3)
+    r2(2, 2)
+    r2(0, 2)
+    r2(2, 3)
+    r2(2, 0)
+    r3(2, 2)
     r2(1, 1)
-    r1(2)
-    r2(1, 0)
+    r2(2, 1)
+    rz1(0)
     r2(0, 1)
-    r2(2, 1)
-    r2(2, 0)
-    r2(0, 0)
+    r3(2, 0)
+    r3(2, 3)
+    rz1(2)
+    r2(0, 3)
+    loads()
+    last(2)
+    rz1(1)
+    rz1(3)
     r3(2, 1)
-    r3(2, 0)
-    rz1(1)
-    rz1(0)
-    loads()
+    last(0)
+    last(3)
     last(1)
-    last(0)
+    fin(3)
+    fin(2)
+    fin(0)
     fin(1)
-    fin(0)
-
-    for o in both:
-        got(FC[o])
-        store(co * half + x * quarter + o)
-    for o in both:
-        got(LC[o])
-        store(co * half + xo * quarter + o)
-    for copy in stores:
-        copy.wait()
+
+    for o in parts:
+        got(FC[o], LC[o])
     for copy in sent:
         copy.wait_send()
+
+
+def collect(values, loads, out, totals, sem):
+    pieces, _, width = values.shape
+    copies = [
+        pltpu.make_async_copy(values.at[q], out.at[:, pl.ds(q * width, width)], sem.at[q]) for q in range(pieces)
+    ]
+    for copy in copies:
+        copy.start()
+    row = lax.broadcasted_iota(jnp.int32, loads.shape, 0)
+    col = lax.broadcasted_iota(jnp.int32, loads.shape, 1)
+    for e in range(totals.shape[0]):
+        totals[e] = jnp.sum(jnp.where((row == 1) & (col == e), loads[...], 0.0)).astype(jnp.int32)
+    for copy in copies:
+        copy.wait()
 
 
 def planned(n_y, n_planes, tokens, expert_ids, gate_weights, live_counts, w_gate, w_up, w_down):
     n_experts = lax.axis_size("expert")
     rows, model = tokens.shape
     hidden = w_gate.shape[2]
-    n_dp, pieces = n_y * n_planes, 8
+    n_dp, pieces = n_y * n_planes, 16
     width, half, quarter = model // pieces, pieces // 2, pieces // 4
     hbm = pl.BlockSpec(memory_space=pl.ANY)
     smem = pl.BlockSpec(memory_space=pltpu.SMEM)
-    return pl.pallas_call(
+    vmem = pl.BlockSpec(memory_space=pltpu.VMEM)
+    values, loads = pl.pallas_call(
         functools.partial(kernel, n_y, n_planes, n_experts),
         name="moe",
-        out_shape=(jax.ShapeDtypeStruct((rows, model), BF16), jax.ShapeDtypeStruct((n_experts,), jnp.int32)),
+        out_shape=(pltpu.VMEM((pieces, rows, width), BF16), pltpu.VMEM((8, rows), F32)),
         in_specs=[hbm] * 3 + [smem] + [hbm] * 3,
-        out_specs=(hbm, smem),
+        out_specs=(vmem, vmem),
         scratch_shapes=[
             pltpu.VMEM((n_dp, pieces, rows, width), BF16),
             pltpu.VMEM((n_dp, 8, rows), F32),
@@ -472,20 +534,28 @@
             pltpu.VMEM((n_planes, n_y * rows, hidden), BF16),
             pltpu.VMEM((n_dp, pieces, rows, width), BF16),
             pltpu.VMEM((n_planes, n_y, half, rows, width), BF16),
-            pltpu.VMEM((n_planes, 2, 2, rows, width), BF16),
-            pltpu.VMEM((2, 2, rows, width), BF16),
-            pltpu.VMEM((2, 2, rows, width), BF16),
-            pltpu.VMEM((2, rows, width), BF16),
-            pltpu.VMEM((2, 2, rows, width), BF16),
-            pltpu.VMEM((pieces, rows, width), BF16),
-            pltpu.SemaphoreType.DMA((128,)),
-            pltpu.SemaphoreType.DMA((128,)),
-            pltpu.SemaphoreType.DMA((32,)),
+            pltpu.VMEM((n_planes, quarter, 2, rows, width), BF16),
+            pltpu.VMEM((2, quarter, rows, width), BF16),
+            pltpu.VMEM((quarter, 2, rows, width), BF16),
+            pltpu.VMEM((quarter, rows, width), BF16),
+            pltpu.VMEM((2, quarter, rows, width), BF16),
+            pltpu.SemaphoreType.DMA((224,)),
+            pltpu.SemaphoreType.DMA((224,)),
+            pltpu.SemaphoreType.DMA((64,)),
         ],
         compiler_params=pltpu.CompilerParams(
-            collective_id=0, has_side_effects=True, vmem_limit_bytes=63 * 2**20
+            collective_id=0, has_side_effects=True, vmem_limit_bytes=56 * 2**20
         ),
     )(tokens, expert_ids.T, gate_weights.T, live_counts, w_gate, w_up, w_down)
+    return pl.pallas_call(
+        collect,
+        name="collect",
+        out_shape=(jax.ShapeDtypeStruct((rows, model), BF16), jax.ShapeDtypeStruct((n_experts,), jnp.int32)),
+        in_specs=[vmem, vmem],
+        out_specs=(hbm, smem),
+        scratch_shapes=[pltpu.SemaphoreType.DMA((pieces,))],
+        compiler_params=pltpu.CompilerParams(vmem_limit_bytes=4 * 2**20),
+    )(values, loads)
 
 
 def solution(mesh):

time: 96.4 us -> 92.5 us (0.960)
  local copies, waits for them, and re-layouts: 3.4 us -> 0 us
    unnamed x2 -> x0, local copies, waits for them, and re-layouts: 3.4 us -> none
    pallas_call x1, Pallas kernels: 91.5 us -> 89.3 us  [planned(): pl.pallas_call(functools.partial(kernel, n_y, n_planes, n_experts), name=...]
    pallas_call x0 -> x1, Pallas kernels: none -> 1.61 us  [planned(): pl.pallas_call(collect, name='collect', out_shape=(jax.ShapeDtypeStruct((...]
where the time goes in v2:
time: 92.5 us; the launch traced here: 92.3 us
  Pallas kernels  90.9 us (98%)
  between operations  1.45 us (2%)
    pallas_call x1, Pallas kernels, planned(): pl.pallas_call(functools.partial(kernel, n_y, n_planes, n_experts), name=...  89.3 us

profile of v2, /device:TPU:9, one launch (start us, length us, event | category | flops | bytes accessed | tf_op | source)
XLA Modules:
  0.0 92.3 jit_solution(5143034842217827363)
XLA Ops:
  1.3 89.3 %moe.1 = (bf16[16,128,256]{2,1,0:T(8,128)(2,1)S(1)}, f32[8,128]{1,0:T(8,128)S(1)}) custom-call(bf16[128,4096]{1,0:T(8,128)(2,1)} %tokens.1, s32[2,128]{1,0:T(2,128)} %bitcast.2, f32[2,128]{1,0:T(2,128)} %bitcast.3, s32[1]{0:T(128)S(6)} %copy.9.live, bf16[1,4096,1024]{2,1,0:T(8,128)(2,1)} %w_gate.1, bf16[1,4096,1024]{2,1,0:T(8,128)(2,1)} %w_up.1, ...), custom_call_target="tpu_custom_call" | custom-call | tf_op jit(solution)/shard_map/moe/pallas_call | solution.py:520
  90.6 1.6 %collect.1 = (bf16[128,4096]{1,0:T(8,128)(2,1)}, s32[4]{0:T(128)}) custom-call(bf16[16,128,256]{2,1,0:T(8,128)(2,1)S(1)} %get-tuple-element.4.values, f32[8,128]{1,0:T(8,128)S(1)} %get-tuple-element.5.loads), custom_call_target="tpu_custom_call" | custom-call | tf_op jit(solution)/shard_map/collect/pallas_call | solution.py:550

commit v3 on v2

--- a/solution.py
+++ b/solution.py
@@ -34,7 +34,7 @@
 
 
 def kernel(n_y, n_planes, n_experts, tokens, ids, gates, live, w_gate, w_up, w_down, OUT, LOADS,
-           G, M, IDS, GATES, WG, WU, WD, H, Y, RC, RT, RS, RZ1, RL, RZ, send_sem, recv_sem, local_sem):
+           G, M, IDS, GATES, WG, WU, WD, H, Y, RC, RT, RS, RZ1, RE, RZ, send_sem, recv_sem, local_sem):
     dp, ex = lax.axis_index("dp"), lax.axis_index("expert")
     z, y = dp // n_y, dp % n_y
     x, c = ex // 2, ex % 2
@@ -104,8 +104,6 @@
         for copy in copies:
             copy.wait_recv()
 
-    mine_c, other_c = pl.ds(c * half, half), pl.ds(co * half, half)
-    P = [[c * half + h * quarter + o for o in range(quarter)] for h in range(2)]
     mx = [c * half + x * quarter + o for o in range(quarter)]
     ox = [c * half + xo * quarter + o for o in range(quarter)]
 
@@ -116,7 +114,7 @@
 
     def halves(k, o, by_y):
         if by_y:
-            return [(rank[k], P[i][o]) for i in both]
+            return [(rank[k], ox[o]), (rank[k], mx[o])]
         return [(member[k][i], mx[o]) for i in both]
 
     def hop(by_y):
@@ -127,7 +125,7 @@
     F1 = [[same(G.at[r, q], hop(y_first[1][o])) for r, q in halves(1, o, y_first[1][o])] for o in parts]
     D1 = [
         [same(G.at[r, q], core_peer) for r, q in halves(1, o, y_first[1][o])]
-        + [same(G.at[other[1], P[i][o]] if y_first[1][o] else G.at[member[1][i], ox[o]], core_peer) for i in both]
+        + [same(G.at[other[1], (ox, mx)[i][o]] if y_first[1][o] else G.at[member[1][i], ox[o]], core_peer) for i in both]
         for o in parts
     ]
     ZS, GX, GY, GH, DZ, DF, DR = [[None, None] for _ in range(7)]
@@ -146,12 +144,19 @@
     ZG = [None, None] + [[arrival(G.at[me, mx[o]], first + (k - 2) * quarter + o) for o in parts] for k in far]
 
     sum_y = [(True, True, False, False), (True, True, False, False), (True, True, False, False), (True, True, False, False)]
-    C = [link(Y.at[pair[k], other_c], RC.at[k], core_peer) for k in range(n_planes)]
+    sides = [xo * quarter, x * quarter]
+    C = [
+        [
+            link(Y.at[pair[k], pl.ds(co * half + side, quarter)], RC.at[k, :, pl.ds(side, quarter)], core_peer)
+            for side in sides
+        ]
+        for k in range(n_planes)
+    ]
     T, TG, S = [], [], [None, None]
     for k in range(n_planes):
         T.append([
             [
-                link(Y.at[other[k], P[i][o]], RT.at[k, o, i], y_peer)
+                link(Y.at[other[k], (ox, mx)[i][o]], RT.at[k, o, i], y_peer)
                 if sum_y[k][o]
                 else link(Y.at[member[k][i], ox[o]], RT.at[k, o, i], x_peer)
                 for i in both
@@ -172,11 +177,13 @@
     ]
     ZA = [[arrival(RZ.at[i, o], start + i * quarter + o) for o in parts] for i in both]
     ZR1 = [[link(Y.at[TG[1][o][i]], RZ1.at[o, i], z_peer[1]) for i in both] for o in parts]
-    L0 = [
-        link(Y.at[me, ox[o]], RL.at[o], x_peer) if sum_y[0][o] else link(Y.at[other[0], mx[o]], RL.at[o], y_peer)
+    E = [
+        [link(Y.at[me, ox[o]], RE.at[o, 0], x_peer), link(Y.at[me, mx[o]], RE.at[o, 1], x_peer)]
+        if sum_y[0][o]
+        else [link(Y.at[other[0], mx[o]], RE.at[o, 0], y_peer), None]
         for o in parts
     ]
-    FX = [same(OUT.at[mx[o]], x_peer) for o in parts]
+    FX = [None if sum_y[0][o] else same(OUT.at[mx[o]], x_peer) for o in parts]
     FC = [same(OUT.at[mx[o]], core_peer) for o in parts]
     LC = [same(OUT.at[ox[o]], core_peer) for o in parts]
 
@@ -250,10 +257,8 @@
             got(*DZ[k], *DF[k], *[copy for o in parts for copy in DR[k][o]])
 
     def tiles(tile, lo, hi):
-        if hi - lo == 1:
-            tile(lo)
-        else:
-            lax.fori_loop(lo, hi, lambda i, carry: (tile(i), carry)[1], 0, unroll=True)
+        for t in range(lo, hi):
+            tile(t)
 
     scales = {}
 
@@ -267,7 +272,7 @@
             scales[k] = jnp.concatenate(columns, axis=0)
 
         def tile(t):
-            cols = pl.ds(t * h_tile if isinstance(t, int) else pl.multiple_of(t * h_tile, h_tile), h_tile)
+            cols = pl.ds(t * h_tile, h_tile)
             lhs = jnp.concatenate([G[pair[k], q].reshape(n_y * rows, width) for q in range(pieces)], axis=1)
             g = jnp.dot(lhs, WG[:, cols], preferred_element_type=F32)
             u = jnp.dot(lhs, WU[:, cols], preferred_element_type=F32)
@@ -283,7 +288,7 @@
         downs.append(k)
 
         def tile(t):
-            q = lax.rem(co * half + per * t, pieces)
+            q = (co, c)[t // 2] * half + sides[t % 2]
             cols = pl.ds(pl.multiple_of(q * width, width), per * width)
             part = jnp.dot(H[k], WD[:, cols], preferred_element_type=F32).astype(BF16)
             for i in range(per):
@@ -294,14 +299,18 @@
     def add(r, q, value):
         Y[r, q] = (Y[r, q].astype(F32) + value.astype(F32)).astype(BF16)
 
-    def r1(k):
-        got(C[k])
+    def r1(k, h):
+        got(C[k][h])
         for j in range(n_y):
-            def tile(q, carry):
-                add(member[k][j], c * half + q, RC[k, j, q])
+            def tile(i, carry):
+                add(member[k][j], c * half + sides[h] + i, RC[k, j, sides[h] + i])
                 return carry
-            lax.fori_loop(0, half, tile, 0)
-        go(*[T[k][o][i] for i in both for o in parts])
+            lax.fori_loop(0, quarter, tile, 0)
+        for o in parts:
+            if sum_y[k][o]:
+                go(T[k][o][h])
+            elif h == 0:
+                go(*T[k][o])
 
     def r2(k, o):
         for i in both:
@@ -321,18 +330,32 @@
         for i in both:
             got(ZR1[o][i])
             add(*TG[0][o][i], RZ1[o, i])
-        go(L0[o])
+            if i == (0 if sum_y[0][o] else 1):
+                go(E[o][0])
 
     def last(o):
-        got(L0[o])
-        total = Y[me, mx[o]].astype(F32) + RL[o].astype(F32)
+        total = Y[me, mx[o]].astype(F32)
+        if not sum_y[0][o]:
+            got(E[o][0])
+            total = total + RE[o, 0].astype(F32)
         got(ZA[0][o], ZA[1][o])
-        OUT[mx[o]] = (total + RZ[0, o].astype(F32) + RZ[1, o].astype(F32)).astype(BF16)
-        go(FX[o], FC[o])
+        total = (total + RZ[0, o].astype(F32) + RZ[1, o].astype(F32)).astype(BF16)
+        if sum_y[0][o]:
+            Y[me, mx[o]] = total
+            go(E[o][1])
+        else:
+            OUT[mx[o]] = total
+            go(FX[o], FC[o])
 
     def fin(o):
-        got(FX[o])
-        go(LC[o])
+        if sum_y[0][o]:
+            for i, q, copy in ((0, mx[o], FC[o]), (1, ox[o], LC[o])):
+                got(E[o][i])
+                OUT[q] = (Y[me, q].astype(F32) + RE[o, i].astype(F32)).astype(BF16)
+                go(copy)
+        else:
+            got(FX[o])
+            go(LC[o])
 
     def loads():
         count = M[0]
@@ -340,152 +363,160 @@
             count = count + M[r]
         LOADS[...] = count
 
+    st(2)
+    st(10)
+    st(0)
+    st(6)
+    st(7)
+    st(1)
+    st(3)
+    st(8)
     st(9)
-    st(2)
-    st(6)
-    st(1)
-    st(0)
-    st(7)
-    st(3)
-    st(10)
-    st(8)
-    a0(3)
     st(4)
     st(11)
+    st(5)
+    st(15)
+    a0(0)
+    st(14)
     a0(2)
-    st(5)
+    a0(1)
+    a0(3)
+    zg(3, 2)
     zg(3, 0)
-    st(14)
-    a0(0)
-    a0(1)
-    zg(3, 2)
+    b0(3)
+    zg(3, 3)
+    b0(0)
+    st(12)
+    b0(1)
     zg(3, 1)
     b0(2)
-    b0(3)
+    whole(0)
+    gh(3, 0)
     gh(3, 2)
-    b0(1)
-    b0(0)
-    whole(0)
-    zg(3, 3)
-    gh(3, 0)
-    gate_up(0, 0, 2)
+    gate_up(0, 0, 1)
+    gh(3, 3)
+    gb(3, 3)
+    fz(3, 1)
+    gb(3, 2)
+    gh(3, 1)
+    fz(0, 0)
+    st(13)
+    gate_up(0, 1, 3)
+    gc(3, 2)
+    fz(0, 1)
+    zg(2, 2)
     zg(2, 0)
     gb(3, 0)
-    st(13)
-    gate_up(0, 2, 3)
-    gh(3, 3)
-    gb(3, 2)
-    gh(3, 1)
-    gc(3, 2)
-    gate_up(0, 3, 4)
-    st(12)
-    st(15)
-    zg(2, 2)
-    down(0, 0, 1)
-    fz(1, 0)
-    gb(3, 3)
+    gc(3, 3)
     fz(3, 0)
     gc(3, 0)
     gb(3, 1)
-    gc(3, 3)
+    gate_up(0, 3, 4)
     gc(3, 1)
-    down(0, 1, 2)
-    go(C[0])
+    whole(3)
+    zg(2, 3)
+    gate_up(3, 0, 2)
+    fz(2, 0)
+    fz(1, 0)
+    gate_up(3, 2, 3)
+    gh(2, 0)
+    f1(0, 0)
+    fz(2, 1)
     fz(1, 1)
-    fz(0, 0)
-    zg(2, 3)
-    whole(3)
-    gate_up(3, 0, 1)
-    fz(2, 1)
-    fz(0, 1)
-    gate_up(3, 1, 2)
-    fz(2, 0)
-    gate_up(3, 2, 3)
-    fz(3, 1)
-    f1(1, 1)
-    gh(2, 0)
+    zg(2, 1)
     gh(2, 2)
     gate_up(3, 3, 4)
-    gh(2, 3)
-    f1(3, 0)
-    down(3, 0, 2)
-    go(C[3])
-    zg(2, 1)
+    down(3, 0, 1)
+    go(C[3][0])
+    down(3, 1, 2)
+    go(C[3][1])
+    f1(0, 1)
     down(3, 2, 3)
     f1(1, 0)
+    f1(2, 0)
+    down(0, 0, 1)
+    go(C[0][0])
+    gh(2, 3)
+    r1(3, 0)
+    f1(3, 0)
+    gb(2, 3)
+    f1(1, 1)
+    down(3, 3, 4)
+    r1(3, 1)
+    f1(3, 1)
+    f1(2, 1)
+    gh(2, 1)
+    down(0, 1, 2)
+    go(C[0][1])
     down(0, 2, 3)
-    f1(2, 1)
-    f1(0, 0)
-    f1(0, 1)
-    f1(2, 0)
-    down(3, 3, 4)
-    r1(3)
-    f1(3, 1)
+    whole(1)
+    gate_up(1, 0, 3)
+    gb(2, 1)
+    r2(3, 2)
     down(0, 3, 4)
+    r2(3, 0)
+    gate_up(1, 3, 4)
     gc(2, 2)
-    whole(1)
-    gate_up(1, 0, 1)
+    gb(2, 2)
+    r1(0, 1)
+    r2(3, 1)
+    r1(0, 0)
+    down(1, 0, 1)
+    go(C[1][0])
+    down(1, 1, 2)
+    go(C[1][1])
+    down(1, 2, 3)
+    gc(2, 3)
     gc(2, 0)
-    gc(2, 3)
-    gh(2, 1)
-    gate_up(1, 1, 4)
-    r2(3, 0)
+    gc(2, 1)
+    r3(3, 2)
+    r1(1, 0)
+    r2(3, 3)
     gb(2, 0)
-    r2(3, 2)
-    down(1, 0, 2)
-    go(C[1])
-    r2(3, 1)
-    gb(2, 1)
-    gb(2, 3)
-    r2(3, 3)
-    down(1, 2, 3)
-    gb(2, 2)
     r3(3, 0)
-    r1(0)
-    gc(2, 1)
     down(1, 3, 4)
-    r1(1)
     whole(2)
-    gate_up(2, 0, 1)
+    r1(1, 1)
+    gate_up(2, 0, 4)
     r3(3, 1)
-    gate_up(2, 1, 3)
-    r3(3, 2)
-    gate_up(2, 3, 4)
-    down(2, 0, 2)
-    go(C[2])
+    down(2, 0, 1)
+    go(C[2][0])
+    down(2, 1, 2)
+    go(C[2][1])
+    r2(1, 2)
+    down(2, 2, 3)
+    r2(1, 0)
+    r1(2, 0)
+    r2(0, 2)
+    down(2, 3, 4)
+    r3(3, 3)
+    r1(2, 1)
+    r2(2, 2)
+    r2(2, 0)
+    r2(2, 1)
+    r2(1, 3)
+    r3(2, 2)
+    r2(2, 3)
+    r3(2, 0)
+    rz1(2)
+    r3(2, 1)
+    r2(1, 1)
+    r2(0, 3)
+    rz1(3)
+    r3(2, 3)
+    r2(0, 1)
     r2(0, 0)
-    down(2, 2, 3)
-    r2(1, 2)
-    down(2, 3, 4)
-    r1(2)
-    r3(3, 3)
-    r2(1, 0)
-    r2(1, 3)
-    r2(2, 2)
-    r2(0, 2)
-    r2(2, 3)
-    r2(2, 0)
-    r3(2, 2)
-    r2(1, 1)
-    r2(2, 1)
     rz1(0)
-    r2(0, 1)
-    r3(2, 0)
-    r3(2, 3)
-    rz1(2)
-    r2(0, 3)
     loads()
     last(2)
+    last(0)
     rz1(1)
-    rz1(3)
-    r3(2, 1)
-    last(0)
+    last(1)
     last(3)
-    last(1)
+    fin(1)
+    fin(0)
+    fin(2)
     fin(3)
-    fin(2)
-    fin(0)
-    fin(1)
 
     for o in parts:
         got(FC[o], LC[o])
@@ -537,7 +568,7 @@
             pltpu.VMEM((n_planes, quarter, 2, rows, width), BF16),
             pltpu.VMEM((2, quarter, rows, width), BF16),
             pltpu.VMEM((quarter, 2, rows, width), BF16),
-            pltpu.VMEM((quarter, rows, width), BF16),
+            pltpu.VMEM((quarter, 2, rows, width), BF16),
             pltpu.VMEM((2, quarter, rows, width), BF16),
             pltpu.SemaphoreType.DMA((224,)),
             pltpu.SemaphoreType.DMA((224,)),

time: 92.5 us -> 91.8 us (level)
  no operation moved by 1% of the time
where the time goes in v3:
time: 91.8 us; the launch traced here: 91.6 us
  Pallas kernels  90.1 us (98%)
  between operations  1.47 us (2%)
    pallas_call x1, Pallas kernels, planned(): pl.pallas_call(functools.partial(kernel, n_y, n_planes, n_experts), name=...  88.5 us

profile of v3, /device:TPU:9, one launch (start us, length us, event | category | flops | bytes accessed | tf_op | source)
XLA Modules:
  0.0 91.6 jit_solution(10980592908327980372)
XLA Ops:
  1.3 88.5 %moe.1 = (bf16[16,128,256]{2,1,0:T(8,128)(2,1)S(1)}, f32[8,128]{1,0:T(8,128)S(1)}) custom-call(bf16[128,4096]{1,0:T(8,128)(2,1)} %tokens.1, s32[2,128]{1,0:T(2,128)} %bitcast.2, f32[2,128]{1,0:T(2,128)} %bitcast.3, s32[1]{0:T(128)S(6)} %copy.9.live, bf16[1,4096,1024]{2,1,0:T(8,128)(2,1)} %w_gate.1, bf16[1,4096,1024]{2,1,0:T(8,128)(2,1)} %w_up.1, ...), custom_call_target="tpu_custom_call" | custom-call | tf_op jit(solution)/shard_map/moe/pallas_call | solution.py:551
  89.8 1.6 %collect.1 = (bf16[128,4096]{1,0:T(8,128)(2,1)}, s32[4]{0:T(128)}) custom-call(bf16[16,128,256]{2,1,0:T(8,128)(2,1)S(1)} %get-tuple-element.4.values, f32[8,128]{1,0:T(8,128)S(1)} %get-tuple-element.5.loads), custom_call_target="tpu_custom_call" | custom-call | tf_op jit(solution)/shard_map/collect/pallas_call | solution.py:581
